TPU v7x, 32 devices: a whole 2x2x4 slice. The times are simulated.
32 devices in a mesh: row: 16 (over z, x, core), col: 2 (over y).
Axes of the slice: x: 2, y: 2, z: 4, core: 2. Of those that a mesh axis runs over, the one named last changes fastest.
Arguments:
- qkv: bfloat16 [256, 16, 3, 3072], P('row', 'col'), may hold values from -6 to 6
- cotangent: bfloat16 [256, 16, 3072], P('row', 'col'), may hold values from -6 to 6
- norm_gains: float32 [2, 128], replicated, may hold values from 0.1 to 1.9
- rel_table: float32 [24, 15, 15], replicated, may hold values from -6 to 250
- shifts: int32 [2], replicated, may hold values from 1 to 7
- mask_ids: int32 [256, 16], replicated, may hold values from 0 to 2
Outputs:
- attention: bfloat16 [256, 16, 3072], P('row', 'col')
- d_qkv: bfloat16 [256, 16, 3, 3072], P('row', 'col')
- d_gains: float32 [2, 128], replicated
- d_table: float32 [24, 15, 15], replicated
All inputs are finite; a program needn't handle non-finite values.
Results may differ from a plain program's by a relative error of at most 0.0073.
Values may be sent and summed in bfloat16 or wider, within the bound.
A program may use at most 192 MiB of HBM per device.

v0:
```python
import functools
import math

import jax
import jax.numpy as jnp
from jax import lax
from jax.experimental import pallas as pl
from jax.experimental.pallas import tpu as pltpu
from jax.sharding import PartitionSpec as P

EPSILON = 1e-06
NEG_FILL = -1e30
MESH = pl.DeviceIdType.MESH
F32 = jnp.float32
BF16 = jnp.bfloat16
LAG_COMPUTE = 4
LAG_ASSEMBLE = 4
LAG_FINAL = 4


def dot(a, b, lhs, rhs):
    return lax.dot_general(a, b, (((lhs,), (rhs,)), ((), ())), preferred_element_type=F32)


def window_kernel(
    steps,
    qkv,
    cot,
    gains,
    table,
    mask,
    att_out,
    dqkv_out,
    dgain,
    dtable,
    own_a,
    own_b,
    rowin_a,
    rowin_b,
    tokens,
    col_send,
    col_recv,
    results,
    out_send,
    out_recv,
    row_send,
    row_recv,
    neg,
    gather,
    scatter,
    gain_sum,
    flat,
    across_table,
    skew,
    sum_send,
    sum_recv,
    load_sem,
    rowin_send_sem,
    rowin_recv_sem,
    col_sems,
    out_sems,
    row_sems,
    sum_sems,
    *,
    row_dir,
    col_dir,
    width,
    win,
    heads,
    dim,
):
    chunks = own_a.shape[0]
    tile_rows, tile_cols = own_a.shape[1], own_a.shape[3]
    lanes = own_a.shape[4]
    half = win // 2
    size = tile_rows * tile_cols
    pad = width * tile_rows
    bands = tile_rows // win
    scale = 1.0 / math.sqrt(dim)
    rows = lax.axis_size("row")
    cols = lax.axis_size("col")
    me_row = lax.axis_index("row")
    me_col = lax.axis_index("col")
    row_step = jnp.where(steps[0] <= half, steps[0], steps[0] - win)
    kept = size - pad

    def row_at(step):
        return (lax.rem(me_row + step + rows, rows), me_col)

    def col_at(step):
        return (me_row, lax.rem(me_col + step + cols, cols))

    def lane(g):
        return pl.ds(pl.multiple_of(g * lanes, lanes), lanes)

    first_row = 0 if row_dir > 0 else tile_rows - half
    halo_rows = pl.ds(first_row, half)

    def loads(g):
        return (
            pltpu.make_async_copy(qkv.at[:, :, :, lane(g)], own_a.at[g], load_sem.at[0, g]),
            pltpu.make_async_copy(cot.at[:, :, lane(g)], own_b.at[g], load_sem.at[1, g]),
        )

    def row_ins(g):
        return (
            pltpu.make_async_remote_copy(
                qkv.at[halo_rows, :, :, lane(g)],
                rowin_a.at[g],
                rowin_send_sem.at[0, g],
                rowin_recv_sem.at[0, g],
                device_id=row_at(-row_dir),
                device_id_type=MESH,
            ),
            pltpu.make_async_remote_copy(
                cot.at[halo_rows, :, lane(g)],
                rowin_b.at[g],
                rowin_send_sem.at[1, g],
                rowin_recv_sem.at[1, g],
                device_id=row_at(-row_dir),
                device_id_type=MESH,
            ),
        )

    def col_in(g):
        return pltpu.make_async_remote_copy(
            col_send.at[g],
            col_recv.at[g],
            col_sems.at[0, g],
            col_sems.at[1, g],
            device_id=col_at(-col_dir),
            device_id_type=MESH,
        )

    def col_back(g):
        return pltpu.make_async_remote_copy(
            out_send.at[g],
            out_recv.at[g],
            out_sems.at[0, g],
            out_sems.at[1, g],
            device_id=col_at(col_dir),
            device_id_type=MESH,
        )

    def row_back(g):
        return pltpu.make_async_remote_copy(
            row_send.at[g],
            row_recv.at[g],
            row_sems.at[0, g],
            row_sems.at[1, g],
            device_id=row_at(row_dir),
            device_id_type=MESH,
        )

    partners = []
    for axis, count, me in (("row", rows, me_row), ("col", cols, me_col)):
        reach = 1
        while reach < count:
            across = me + reach - 2 * reach * ((me // reach) % 2)
            partners.append((across, me_col) if axis == "row" else (me_row, across))
            reach *= 2

    def sum_copy(k):
        return pltpu.make_async_remote_copy(
            sum_send.at[k],
            sum_recv.at[k],
            sum_sems.at[0, k],
            sum_sems.at[1, k],
            device_id=partners[k],
            device_id_type=MESH,
        )

    @pl.loop(0, chunks)
    def _(g):
        for copy in loads(g):
            copy.start()

    barrier = pltpu.get_barrier_semaphore()
    row_rounds = rows.bit_length() - 1
    greeted = [row_at(1), row_at(-1), col_at(1)] + ([col_at(-1)] if cols > 2 else [])
    greeted += partners[1:row_rounds] + partners[row_rounds + 1 :]
    for neighbour in greeted:
        pl.semaphore_signal(barrier, inc=1, device_id=neighbour, device_id_type=MESH)
    pl.semaphore_wait(barrier, len(greeted))

    @pl.loop(0, chunks)
    def _(g):
        for copy in row_ins(g):
            copy.start()

    gain_sum[...] = jnp.zeros_like(gain_sum)
    span = table.shape[0]
    shift = (win - 1) * (tile_rows + 1)
    head_count = chunks * heads

    def spot_of(x, y):
        return (span - 1 - y) * tile_rows + span - 1 - x

    flat[...] = jnp.zeros_like(flat)

    @pl.loop(0, span)
    def _(x):
        for y in range(span):
            flat[pl.ds(spot_of(x, y), 1), 0:head_count] = table[x, y : y + 1, :]

    turned = jnp.concatenate([flat[:size].T, flat[size:].T], axis=1)
    across_table[...] = pltpu.roll(turned, 2 * size - shift, 1)

    iota = functools.partial(lax.broadcasted_iota, jnp.int32)

    def column_of(slot):
        if col_dir > 0:
            return jnp.where(slot < tile_cols - width, slot + width, slot - (tile_cols - width))
        return slot

    reach = size + half * tile_cols
    slot, source = iota((size, reach), 0), iota((size, reach), 1)
    row = slot % tile_rows + row_step
    column = column_of(slot // tile_rows)
    if row_dir > 0:
        wanted = row
    else:
        wanted = jnp.where(row < 0, row + half + tile_rows, row)
    gather[...] = (source == wanted * tile_cols + column).astype(BF16)
    spot, slot = iota((size, size), 0), iota((size, size), 1)
    row = (slot % tile_rows + row_step + tile_rows) % tile_rows
    scatter[...] = (spot == row * tile_cols + column_of(slot // tile_rows)).astype(BF16)

    row_count, col_count = mask.shape[1], mask.shape[0]
    from_row = lax.rem(row_count + me_row * tile_rows + row_step, row_count)
    from_col = lax.rem(col_count + me_col * tile_cols + jnp.where(steps[1] <= half, steps[1], steps[1] - win), col_count)
    pick = (from_row + iota((row_count, size), 1) % tile_rows) % row_count
    pick = (iota((row_count, size), 0) == pick).astype(F32)
    by_row = dot(mask[...].astype(F32), pick, 1, 0)
    pick = (from_col + iota((col_count, size), 1) // tile_rows) % col_count
    across = jnp.where(iota((col_count, size), 0) == pick, by_row, 0.0)
    across = jnp.sum(across, axis=0, keepdims=True)
    band = (iota((1, size), 1) % tile_rows) // win
    code = jnp.broadcast_to(across * bands + band.astype(F32), (size, size))
    neg[...] = jnp.where(code == code.T, 0.0, NEG_FILL)

    gain_q, gain_k = gains[0:1, :], gains[1:2, :]
    head_lanes = [pl.ds(i * dim, dim) for i in range(heads)]

    def merge(g):
        for copy in loads(g):
            copy.wait()
        for copy in row_ins(g):
            copy.wait_recv()
        for f in range(4):
            own = own_a[g, :, f] if f < 3 else own_b[g]
            halo = rowin_a[g, :, f] if f < 3 else rowin_b[g]
            tiles = [own[r].astype(F32) for r in range(tile_rows)]
            tiles += [halo[r].astype(F32) for r in range(half)]
            placed = dot(gather[...], jnp.concatenate(tiles, axis=0).astype(BF16), 1, 0)
            placed = placed.astype(BF16)
            tokens[g, f] = placed[:kept]
            col_send[g, f] = placed[kept:]
        col_in(g).start()

    def normed(x, gain):
        centred = x - jnp.mean(x, axis=-1, keepdims=True)
        variance = jnp.mean(centred * centred, axis=-1, keepdims=True)
        inv = lax.rsqrt(variance + EPSILON)
        hat = centred * inv
        return hat, inv, (hat * gain).astype(BF16)

    def norm_back(hat, inv, dn, gain):
        g = dn * gain
        first = jnp.mean(g, axis=-1, keepdims=True)
        second = jnp.mean(g * hat, axis=-1, keepdims=True)
        return inv * (g - first - hat * second), jnp.sum(dn * hat, axis=0, keepdims=True)

    sub = 8
    lane_at = lax.broadcasted_iota(jnp.int32, (sub, size), 1)

    def attend(g, i):
        at = head_lanes[i]
        head = g * heads + i
        pairs = [(tokens[g, f, :, at], col_recv[g, f, :, at]) for f in range(4)]
        q, k, v, ct = [jnp.concatenate(pair[::col_dir], axis=0) for pair in pairs]
        q_hat, q_inv, qn = normed(q.astype(F32), gain_q)
        k_hat, k_inv, kn = normed(k.astype(F32), gain_k)
        base = jnp.broadcast_to(across_table[pl.ds(head, 1), :], (sub, 2 * size))
        base = pltpu.roll(base, 0, 1, stride=1, stride_axis=0)
        low, high = base[:, :size], base[:, size:]
        blocks = []
        for b in range(size // sub):
            if b == 0:
                blocks.append(low)
            else:
                blocks.append(
                    jnp.where(
                        lane_at < b * sub,
                        pltpu.roll(high, b * sub, 1),
                        pltpu.roll(low, b * sub, 1),
                    )
                )
        bias = jnp.concatenate(blocks, axis=0)
        s = dot(qn, kn, 1, 1) * scale + bias + neg[...]
        e = jnp.exp(s - jnp.max(s, axis=-1, keepdims=True))
        p = e * (1.0 / jnp.sum(e, axis=-1, keepdims=True))
        pb = p.astype(BF16)
        att = dot(pb, v, 1, 0)
        dp = dot(ct, v, 1, 1)
        ds = p * (dp - jnp.sum(p * dp, axis=-1, keepdims=True))
        dsb = ds.astype(BF16)
        dqn = dot(dsb, kn, 1, 0) * scale
        dkn = dot(dsb, qn, 0, 0) * scale
        dv = dot(pb, ct, 0, 0)
        low, high = ds[:sub], jnp.zeros((sub, size), F32)
        for b in range(1, size // sub):
            moved = pltpu.roll(ds[b * sub : (b + 1) * sub], size - b * sub, 1)
            inside = lane_at < size - b * sub
            low = low + jnp.where(inside, moved, 0.0)
            high = high + jnp.where(inside, 0.0, moved)
        skew[0, pl.ds(head * sub, sub), :] = low
        skew[1, pl.ds(head * sub, sub), :] = high
        dq, gq = norm_back(q_hat, q_inv, dqn, gain_q)
        dk, gk = norm_back(k_hat, k_inv, dkn, gain_k)
        for f, value in enumerate((att, dq, dk, dv)):
            value = value.astype(BF16)
            if col_dir > 0:
                results[g, f, :, at] = value[:kept]
                out_send[g, f, :, at] = value[kept:]
            else:
                out_send[g, f, :, at] = value[:pad]
                results[g, f, :, at] = value[pad:]
        return jnp.concatenate([gq, gk], axis=0)

    def compute(g):
        col_in(g).wait_recv()
        parts = [attend(g, i) for i in range(heads)]
        gain_sum[...] += functools.reduce(jnp.add, parts)
        col_back(g).start()

    def assemble(g):
        col_back(g).wait_recv()
        for f in range(4):
            value = jnp.concatenate([results[g, f], out_recv[g, f]], axis=0)
            value = dot(scatter[...], value, 1, 0)
            for r in range(tile_rows):
                tile = value[r * tile_cols : (r + 1) * tile_cols].astype(BF16)
                if first_row <= r < first_row + half:
                    row_send[g, r - first_row, f] = tile
                elif f == 0:
                    att_out[r, :, lane(g)] = tile
                else:
                    dqkv_out[r, f - 1, :, lane(g)] = tile
        row_back(g).start()

    def final(g):
        row_back(g).wait_recv()
        for f in range(4):
            for j in range(half):
                r = first_row + j
                foreign = (r < row_step) if row_dir > 0 else (r >= tile_rows + row_step)
                tile = jnp.where(
                    foreign, row_recv[g, j, f].astype(F32), row_send[g, j, f].astype(F32)
                ).astype(BF16)
                if f == 0:
                    att_out[r, :, lane(g)] = tile
                else:
                    dqkv_out[r, f - 1, :, lane(g)] = tile

    def first_sum():
        total = jnp.zeros((head_count, 2 * size), F32)
        for j in range(sub):
            part = [skew[i, pl.ds(j, head_count, stride=sub), :] for i in range(2)]
            part = jnp.concatenate(part, axis=1)
            total = total + (pltpu.roll(part, 2 * size - j, 1) if j else part)
        total = pltpu.roll(total, shift, 1)
        gain = jnp.concatenate([gain_sum[0:1, :], gain_sum[1:2, :]], axis=1)
        rest = jnp.zeros((sum_send.shape[1] - head_count - 1, 2 * size), F32)
        sum_send[0] = jnp.concatenate([total, gain, rest], axis=0)
        sum_copy(0).start()

    def next_sum(k):
        sum_copy(k - 1).wait_recv()
        total = sum_send[k - 1] + sum_recv[k - 1]
        if k < len(partners):
            sum_send[k] = total
            sum_copy(k).start()
            return
        dgain[0:1, :] = total[head_count : head_count + 1, :dim]
        dgain[1:2, :] = total[head_count : head_count + 1, dim:]
        square = jnp.concatenate(
            [total, jnp.zeros((size - total.shape[0], 2 * size), F32)], axis=0
        )
        flat[0:size, :] = square[:, :size].T
        flat[size : 2 * size, :] = square[:, size:].T

        @pl.loop(0, span)
        def _(x):
            for y in range(span):
                dtable[x, y : y + 1, :] = flat[pl.ds(spot_of(x, y), 1), 0:head_count]

    lag_a = min(LAG_COMPUTE, chunks)
    lag_b = lag_a + LAG_ASSEMBLE
    lag_c = lag_b + LAG_FINAL

    rounds = len(partners)
    done = chunks + lag_a

    @pl.loop(0, max(chunks + lag_c, done + rounds + 1))
    def _(t):
        @pl.when(t < chunks)
        def _():
            merge(t)

        @pl.when(jnp.logical_and(t >= lag_c, t < chunks + lag_c))
        def _():
            final(t - lag_c)

        @pl.when(jnp.logical_and(t >= lag_b, t < chunks + lag_b))
        def _():
            assemble(t - lag_b)

        @pl.when(jnp.logical_and(t >= lag_a, t < chunks + lag_a))
        def _():
            compute(t - lag_a)

        for k in range(rounds + 1):

            @pl.when(t == done - 1 + k)
            def _(k=k):
                if k == 0:
                    first_sum()
                else:
                    next_sum(k)

    @pl.loop(0, chunks)
    def _(g):
        for copy in row_ins(g):
            copy.wait_send()
        col_in(g).wait_send()
        col_back(g).wait_send()
        row_back(g).wait_send()

    for k in range(rounds):
        sum_copy(k).wait_send()


def window_pass(
    steps, qkv, cot, gains, table, mask, *, row_dir, col_dir, width, win, dim, call_id
):
    tile_rows, fields, tile_cols, features = qkv.shape
    head_count = features // dim
    heads = 2 if head_count % 2 == 0 else 1
    lanes = heads * dim
    chunks = head_count // heads
    half = win // 2
    size = tile_rows * tile_cols
    pad = width * tile_rows
    rounds = sum(lax.axis_size(a).bit_length() - 1 for a in ("row", "col"))
    sum_rows = -(-(head_count + 1) // 8) * 8
    any_spec = pl.BlockSpec(memory_space=pl.ANY)
    vmem_spec = pl.BlockSpec(memory_space=pltpu.VMEM)
    vmem = pltpu.VMEM
    dma = pltpu.SemaphoreType.DMA
    return pl.pallas_call(
        functools.partial(
            window_kernel,
            row_dir=row_dir,
            col_dir=col_dir,
            width=width,
            win=win,
            heads=heads,
            dim=dim,
        ),
        in_specs=[pl.BlockSpec(memory_space=pltpu.SMEM), any_spec, any_spec]
        + [vmem_spec] * 3,
        out_specs=[vmem_spec] * 4,
        out_shape=[
            jax.ShapeDtypeStruct(cot.shape, BF16),
            jax.ShapeDtypeStruct(qkv.shape, BF16),
            jax.ShapeDtypeStruct((2, dim), F32),
            jax.ShapeDtypeStruct(table.shape, F32),
        ],
        scratch_shapes=[
            vmem((chunks, tile_rows, fields, tile_cols, lanes), BF16),
            vmem((chunks, tile_rows, tile_cols, lanes), BF16),
            vmem((chunks, half, fields, tile_cols, lanes), BF16),
            vmem((chunks, half, tile_cols, lanes), BF16),
            vmem((chunks, 4, size - pad, lanes), BF16),
            vmem((chunks, 4, pad, lanes), BF16),
            vmem((chunks, 4, pad, lanes), BF16),
            vmem((chunks, 4, size - pad, lanes), BF16),
            vmem((chunks, 4, pad, lanes), BF16),
            vmem((chunks, 4, pad, lanes), BF16),
            vmem((chunks, half, 4, tile_cols, lanes), BF16),
            vmem((chunks, half, 4, tile_cols, lanes), BF16),
            vmem((size, size), F32),
            vmem((size, size + half * tile_cols), BF16),
            vmem((size, size), BF16),
            vmem((2, dim), F32),
            vmem((2 * size, size), F32),
            vmem((size, 2 * size), F32),
            vmem((2, head_count * 8, size), F32),
            vmem((rounds, sum_rows, 2 * size), F32),
            vmem((rounds, sum_rows, 2 * size), F32),
            dma((2, chunks)),
            dma((2, chunks)),
            dma((2, chunks)),
            dma((2, chunks)),
            dma((2, chunks)),
            dma((2, chunks)),
            dma((2, rounds)),
        ],
        compiler_params=pltpu.CompilerParams(
            collective_id=call_id, has_side_effects=True, vmem_limit_bytes=60 * 1024 * 1024
        ),
        name="windows",
    )(steps, qkv, cot, gains, table, mask)


def local(qkv, cotangent, norm_gains, rel_table, shifts, mask_ids):
    head_count, span, _ = rel_table.shape
    dim = qkv.shape[3] // head_count
    win = (span + 1) // 2
    half = win // 2
    branches = []
    for row_dir in (1, -1):
        for col_step in (*range(1, half + 1), *range(1 - half, 0)):
            branches.append(
                functools.partial(
                    window_pass,
                    row_dir=row_dir,
                    col_dir=1 if col_step > 0 else -1,
                    width=abs(col_step),
                    win=win,
                    dim=dim,
                    call_id=len(branches),
                )
            )
    index = jnp.where(shifts[0] <= half, 0, win - 1) + shifts[1] - 1
    att, dqkv, dgain, dtable = lax.switch(
        index,
        branches,
        shifts,
        qkv.transpose(0, 2, 1, 3),
        cotangent,
        norm_gains,
        rel_table.transpose(1, 2, 0),
        mask_ids.T,
    )
    return (att, dqkv.transpose(0, 2, 1, 3), dgain, dtable.transpose(2, 0, 1))


def solution(mesh):
    placed = (P("row", "col", None, None), P("row", "col", None), P(), P(), P(), P())
    return jax.shard_map(
        local,
        mesh=mesh,
        in_specs=placed,
        out_specs=(P("row", "col", None), P("row", "col", None, None), P(), P()),
        check_vma=False,
    )
```

profile of v0, /device:TPU:0, one launch (start us, length us, event | category | flops | bytes accessed | tf_op | source)
XLA Modules:
  0.0 64.9 jit_solution(4479897859445366064)
XLA Ops:
  0.6 1.3 %fusion = (s32[1]{0:T(128)}, s32[1]{0:T(128)}) fusion(s32[2]{0:T(128)} %param.24), kind=kLoop, calls=%fused_computation | loop fusion | bytes 16 | tf_op jit(solution)/shard_map/slice | solution.py:536
  3.2 58.1 %conditional.1 = ((bf16[16,8,3072]{2,1,0:T(8,128)(2,1)S(1)}, bf16[16,3,8,3072]{3,2,1,0:T(8,128)(2,1)S(1)}, f32[2,128]{1,0:T(2,128)S(1)}, f32[15,15,24]{2,1,0:T(8,128)S(1)})) conditional(s32[]{:T(128)} %bitcast, (s32[2]{0:T(128)}, bf16[16,3,8,3072]{3,2,1,0:T(8,128)(2,1)}, bf16[16,8,3072]{2,1,0:T(8,128)(2,1)}, ...), branch_computations={%region_0.1_spmd, %region_1.2_spmd, %region_2.3_spmd, %region_3.4_... | conditional | bytes 8 | solution.py:537
  3.8 57.3 %windows.26 = (bf16[16,8,3072]{2,1,0:T(8,128)(2,1)S(1)}, bf16[16,3,8,3072]{3,2,1,0:T(8,128)(2,1)S(1)}, f32[2,128]{1,0:T(2,128)S(1)}, f32[15,15,24]{2,1,0:T(8,128)S(1)}) custom-call(s32[2]{0:T(128)} %get-tuple-element.240.steps, bf16[16,3,8,3072]{3,2,1,0:T(8,128)(2,1)} %get-tuple-element.241.qkv, bf16[16,8,3072]{2,1,0:T(8,128)(2,1)} %get-tuple-element.242.cot, ...), custom_call_target="tpu_custom_call" | custom-call | tf_op jit(solution)/shard_map/cond/branch_12_fun/windows/pallas_call | solution.py:461
  61.4 0.9 %copy.70 = bf16[16,8,3072]{2,1,0:T(8,128)(2,1)} copy(bf16[16,8,3072]{2,1,0:T(8,128)(2,1)S(1)} %get-tuple-element.326) | data formatting | bytes 1572864
  62.3 1.4 %copy.71 = bf16[16,8,3,3072]{3,1,2,0:T(8,128)(2,1)} copy(bf16[16,8,3,3072]{3,1,2,0:T(8,128)(2,1)S(1)} %bitcast.48) | data formatting | bytes 4718592
  63.7 0.6 copy.72
  64.2 0.6 copy.73
where the time goes:
time: 65.3 us; the launch traced here: 64.9 us
  Pallas kernels  57.3 us (88%)
  local copies, waits for them, and re-layouts  4.81 us (7%)
  between operations  1.95 us (3%)
  loops' own time  0.84 us (1%)
    pallas_call x1, Pallas kernels, window_pass(): pl.pallas_call(functools.partial(window_kernel, row_dir=row_dir, col_dir=...  57.3 us
    unnamed x4, local copies, waits for them, and re-layouts  3.5 us
    slice x1, local copies, waits for them, and re-layouts, local(): index = jnp.where(shifts[0] <= half, 0, win - 1) + shifts[1] - 1  1.31 us

commit v1 on v0

--- a/solution.py
+++ b/solution.py
@@ -13,8 +13,9 @@
 MESH = pl.DeviceIdType.MESH
 F32 = jnp.float32
 BF16 = jnp.bfloat16
-LAG_COMPUTE = 4
-LAG_ASSEMBLE = 4
+HEADS = 2
+LAG_COMPUTE = 3
+LAG_RETURN = 3
 LAG_FINAL = 4
 
 
@@ -35,18 +36,22 @@
     dtable,
     own_a,
     own_b,
-    rowin_a,
-    rowin_b,
     tokens,
     col_send,
     col_recv,
-    results,
-    out_send,
-    out_recv,
     row_send,
     row_recv,
+    results,
+    row_out,
+    row_got,
+    col_out,
+    col_got,
     neg,
+    split,
+    strip,
     gather,
+    strip_out,
+    scatter_col,
     scatter,
     gain_sum,
     flat,
@@ -55,11 +60,10 @@
     sum_send,
     sum_recv,
     load_sem,
-    rowin_send_sem,
-    rowin_recv_sem,
     col_sems,
-    out_sems,
     row_sems,
+    row_out_sems,
+    col_out_sems,
     sum_sems,
     *,
     row_dir,
@@ -94,7 +98,6 @@
         return pl.ds(pl.multiple_of(g * lanes, lanes), lanes)
 
     first_row = 0 if row_dir > 0 else tile_rows - half
-    halo_rows = pl.ds(first_row, half)
 
     def loads(g):
         return (
@@ -102,55 +105,23 @@
             pltpu.make_async_copy(cot.at[:, :, lane(g)], own_b.at[g], load_sem.at[1, g]),
         )
 
-    def row_ins(g):
-        return (
-            pltpu.make_async_remote_copy(
-                qkv.at[halo_rows, :, :, lane(g)],
-                rowin_a.at[g],
-                rowin_send_sem.at[0, g],
-                rowin_recv_sem.at[0, g],
-                device_id=row_at(-row_dir),
+    def remote(source, target, sems, device):
+        def copy(g):
+            return pltpu.make_async_remote_copy(
+                source.at[g],
+                target.at[g],
+                sems.at[0, g],
+                sems.at[1, g],
+                device_id=device,
                 device_id_type=MESH,
-            ),
-            pltpu.make_async_remote_copy(
-                cot.at[halo_rows, :, lane(g)],
-                rowin_b.at[g],
-                rowin_send_sem.at[1, g],
-                rowin_recv_sem.at[1, g],
-                device_id=row_at(-row_dir),
-                device_id_type=MESH,
-            ),
-        )
-
-    def col_in(g):
-        return pltpu.make_async_remote_copy(
-            col_send.at[g],
-            col_recv.at[g],
-            col_sems.at[0, g],
-            col_sems.at[1, g],
-            device_id=col_at(-col_dir),
-            device_id_type=MESH,
-        )
-
-    def col_back(g):
-        return pltpu.make_async_remote_copy(
-            out_send.at[g],
-            out_recv.at[g],
-            out_sems.at[0, g],
-            out_sems.at[1, g],
-            device_id=col_at(col_dir),
-            device_id_type=MESH,
-        )
-
-    def row_back(g):
-        return pltpu.make_async_remote_copy(
-            row_send.at[g],
-            row_recv.at[g],
-            row_sems.at[0, g],
-            row_sems.at[1, g],
-            device_id=row_at(row_dir),
-            device_id_type=MESH,
-        )
+            )
+
+        return copy
+
+    col_in = remote(col_send, col_recv, col_sems, col_at(-col_dir))
+    row_in = remote(row_send, row_recv, row_sems, row_at(-row_dir))
+    row_back = remote(row_out, row_got, row_out_sems, row_at(row_dir))
+    col_back = remote(col_out, col_got, col_out_sems, col_at(col_dir))
 
     partners = []
     for axis, count, me in (("row", rows, me_row), ("col", cols, me_col)):
@@ -183,10 +154,26 @@
         pl.semaphore_signal(barrier, inc=1, device_id=neighbour, device_id_type=MESH)
     pl.semaphore_wait(barrier, len(greeted))
 
+    iota = functools.partial(lax.broadcasted_iota, jnp.int32)
+    to, at = iota((size, size), 0), iota((size, size), 1)
+    column = to // tile_rows
+    if col_dir > 0:
+        kept_columns = tile_cols - width
+        column = jnp.where(column < kept_columns, column + width, column - kept_columns)
+    split[...] = (at == (to % tile_rows) * tile_cols + column).astype(BF16)
+
     @pl.loop(0, chunks)
     def _(g):
-        for copy in row_ins(g):
-            copy.start()
+        for copy in loads(g):
+            copy.wait()
+        for f in range(4):
+            own = own_a[g, :, f] if f < 3 else own_b[g]
+            tiles = [own[r].astype(F32) for r in range(tile_rows)]
+            placed = dot(split[...], jnp.concatenate(tiles, axis=0).astype(BF16), 1, 0)
+            placed = placed.astype(BF16)
+            tokens[g, f] = placed[:kept]
+            col_send[g, f] = placed[kept:]
+        col_in(g).start()
 
     gain_sum[...] = jnp.zeros_like(gain_sum)
     span = table.shape[0]
@@ -206,25 +193,49 @@
     turned = jnp.concatenate([flat[:size].T, flat[size:].T], axis=1)
     across_table[...] = pltpu.roll(turned, 2 * size - shift, 1)
 
-    iota = functools.partial(lax.broadcasted_iota, jnp.int32)
-
-    def column_of(slot):
-        if col_dir > 0:
-            return jnp.where(slot < tile_cols - width, slot + width, slot - (tile_cols - width))
-        return slot
-
-    reach = size + half * tile_cols
-    slot, source = iota((size, reach), 0), iota((size, reach), 1)
-    row = slot % tile_rows + row_step
-    column = column_of(slot // tile_rows)
-    if row_dir > 0:
-        wanted = row
+    slots = half * tile_cols
+
+    def is_foreign(r):
+        return (r < row_step) if row_dir > 0 else (r >= tile_rows + row_step)
+
+    to, at = iota((slots, size), 0), iota((slots, size), 1)
+    column, row = to // half, to % half + first_row
+    strip[...] = (at == column * tile_rows + row).astype(BF16)
+    row = (row - row_step + tile_rows) % tile_rows
+    strip_out[...] = (at == column * tile_rows + row).astype(BF16)
+
+    to, at = iota((size, size + slots), 0), iota((size, size + slots), 1)
+    column, row = to // tile_rows, to % tile_rows + row_step
+    halo = row - tile_rows if row_dir > 0 else row + half
+    outside = (row >= tile_rows) if row_dir > 0 else (row < 0)
+    wanted = jnp.where(outside, size + column * half + halo, column * tile_rows + row)
+    gather[...] = (at == wanted).astype(BF16)
+
+    skip = tile_cols - width if col_dir > 0 else 0
+    to, at = iota((pad, pad + slots), 0), iota((pad, pad + slots), 1)
+    column, row = to // tile_rows, to % tile_rows
+    wanted = jnp.where(
+        is_foreign(row),
+        pad + (column + skip) * half + row - first_row,
+        column * tile_rows + (row - row_step + tile_rows) % tile_rows,
+    )
+    scatter_col[...] = (at == wanted).astype(BF16)
+
+    to, at = iota((size, size + slots), 0), iota((size, size + slots), 1)
+    row, column = to // tile_cols, to % tile_cols
+    if col_dir > 0:
+        kept_column, held = column - width, column >= width
+        back_column, place_column = column, column - width
     else:
-        wanted = jnp.where(row < 0, row + half + tile_rows, row)
-    gather[...] = (source == wanted * tile_cols + column).astype(BF16)
-    spot, slot = iota((size, size), 0), iota((size, size), 1)
-    row = (slot % tile_rows + row_step + tile_rows) % tile_rows
-    scatter[...] = (spot == row * tile_cols + column_of(slot // tile_rows)).astype(BF16)
+        kept_column, held = column, column < tile_cols - width
+        back_column, place_column = column - (tile_cols - width), column + width
+    wanted = jnp.where(
+        is_foreign(row),
+        kept + place_column * half + row - first_row,
+        kept_column * tile_rows + (row - row_step + tile_rows) % tile_rows,
+    )
+    wanted = jnp.where(held, wanted, kept + slots + back_column * tile_rows + row)
+    scatter[...] = (at == wanted).astype(BF16)
 
     row_count, col_count = mask.shape[1], mask.shape[0]
     from_row = lax.rem(row_count + me_row * tile_rows + row_step, row_count)
@@ -242,21 +253,16 @@
     gain_q, gain_k = gains[0:1, :], gains[1:2, :]
     head_lanes = [pl.ds(i * dim, dim) for i in range(heads)]
 
+    def in_place(kept_part, other):
+        pair = (kept_part, other)
+        return jnp.concatenate(pair[::col_dir], axis=0)
+
     def merge(g):
-        for copy in loads(g):
-            copy.wait()
-        for copy in row_ins(g):
-            copy.wait_recv()
+        col_in(g).wait_recv()
         for f in range(4):
-            own = own_a[g, :, f] if f < 3 else own_b[g]
-            halo = rowin_a[g, :, f] if f < 3 else rowin_b[g]
-            tiles = [own[r].astype(F32) for r in range(tile_rows)]
-            tiles += [halo[r].astype(F32) for r in range(half)]
-            placed = dot(gather[...], jnp.concatenate(tiles, axis=0).astype(BF16), 1, 0)
-            placed = placed.astype(BF16)
-            tokens[g, f] = placed[:kept]
-            col_send[g, f] = placed[kept:]
-        col_in(g).start()
+            both = in_place(tokens[g, f], col_recv[g, f])
+            row_send[g, f] = dot(strip[...], both, 1, 0).astype(BF16)
+        row_in(g).start()
 
     def normed(x, gain):
         centred = x - jnp.mean(x, axis=-1, keepdims=True)
@@ -274,11 +280,10 @@
     sub = 8
     lane_at = lax.broadcasted_iota(jnp.int32, (sub, size), 1)
 
-    def attend(g, i):
+    def attend(g, i, fields):
         at = head_lanes[i]
         head = g * heads + i
-        pairs = [(tokens[g, f, :, at], col_recv[g, f, :, at]) for f in range(4)]
-        q, k, v, ct = [jnp.concatenate(pair[::col_dir], axis=0) for pair in pairs]
+        q, k, v, ct = [field[:, i * dim : (i + 1) * dim] for field in fields]
         q_hat, q_inv, qn = normed(q.astype(F32), gain_q)
         k_hat, k_inv, kn = normed(k.astype(F32), gain_k)
         base = jnp.broadcast_to(across_table[pl.ds(head, 1), :], (sub, 2 * size))
@@ -319,45 +324,40 @@
         dq, gq = norm_back(q_hat, q_inv, dqn, gain_q)
         dk, gk = norm_back(k_hat, k_inv, dkn, gain_k)
         for f, value in enumerate((att, dq, dk, dv)):
-            value = value.astype(BF16)
-            if col_dir > 0:
-                results[g, f, :, at] = value[:kept]
-                out_send[g, f, :, at] = value[kept:]
-            else:
-                out_send[g, f, :, at] = value[:pad]
-                results[g, f, :, at] = value[pad:]
+            results[g, f, :, at] = value.astype(BF16)
         return jnp.concatenate([gq, gk], axis=0)
 
     def compute(g):
-        col_in(g).wait_recv()
-        parts = [attend(g, i) for i in range(heads)]
+        row_in(g).wait_recv()
+        fields = []
+        for f in range(4):
+            both = in_place(tokens[g, f], col_recv[g, f])
+            both = jnp.concatenate([both, row_recv[g, f]], axis=0)
+            fields.append(dot(gather[...], both, 1, 0).astype(BF16))
+        parts = [attend(g, i, fields) for i in range(heads)]
         gain_sum[...] += functools.reduce(jnp.add, parts)
+        for f in range(4):
+            row_out[g, f] = dot(strip_out[...], results[g, f], 1, 0).astype(BF16)
+        row_back(g).start()
+
+    ours, theirs = pl.ds(0, kept), pl.ds(kept, pad)
+    if col_dir < 0:
+        ours, theirs = pl.ds(pad, kept), pl.ds(0, pad)
+
+    def give_back(g):
+        row_back(g).wait_recv()
+        for f in range(4):
+            both = jnp.concatenate([results[g, f, theirs], row_got[g, f]], axis=0)
+            col_out[g, f] = dot(scatter_col[...], both, 1, 0).astype(BF16)
         col_back(g).start()
 
-    def assemble(g):
+    def final(g):
         col_back(g).wait_recv()
         for f in range(4):
-            value = jnp.concatenate([results[g, f], out_recv[g, f]], axis=0)
-            value = dot(scatter[...], value, 1, 0)
+            parts = [results[g, f, ours], row_got[g, f], col_got[g, f]]
+            value = dot(scatter[...], jnp.concatenate(parts, axis=0), 1, 0)
             for r in range(tile_rows):
                 tile = value[r * tile_cols : (r + 1) * tile_cols].astype(BF16)
-                if first_row <= r < first_row + half:
-                    row_send[g, r - first_row, f] = tile
-                elif f == 0:
-                    att_out[r, :, lane(g)] = tile
-                else:
-                    dqkv_out[r, f - 1, :, lane(g)] = tile
-        row_back(g).start()
-
-    def final(g):
-        row_back(g).wait_recv()
-        for f in range(4):
-            for j in range(half):
-                r = first_row + j
-                foreign = (r < row_step) if row_dir > 0 else (r >= tile_rows + row_step)
-                tile = jnp.where(
-                    foreign, row_recv[g, j, f].astype(F32), row_send[g, j, f].astype(F32)
-                ).astype(BF16)
                 if f == 0:
                     att_out[r, :, lane(g)] = tile
                 else:
@@ -396,7 +396,7 @@
                 dtable[x, y : y + 1, :] = flat[pl.ds(spot_of(x, y), 1), 0:head_count]
 
     lag_a = min(LAG_COMPUTE, chunks)
-    lag_b = lag_a + LAG_ASSEMBLE
+    lag_b = lag_a + LAG_RETURN
     lag_c = lag_b + LAG_FINAL
 
     rounds = len(partners)
@@ -408,17 +408,17 @@
         def _():
             merge(t)
 
+        @pl.when(jnp.logical_and(t >= lag_b, t < chunks + lag_b))
+        def _():
+            give_back(t - lag_b)
+
+        @pl.when(jnp.logical_and(t >= lag_a, t < chunks + lag_a))
+        def _():
+            compute(t - lag_a)
+
         @pl.when(jnp.logical_and(t >= lag_c, t < chunks + lag_c))
         def _():
             final(t - lag_c)
-
-        @pl.when(jnp.logical_and(t >= lag_b, t < chunks + lag_b))
-        def _():
-            assemble(t - lag_b)
-
-        @pl.when(jnp.logical_and(t >= lag_a, t < chunks + lag_a))
-        def _():
-            compute(t - lag_a)
 
         for k in range(rounds + 1):
 
@@ -431,11 +431,8 @@
 
     @pl.loop(0, chunks)
     def _(g):
-        for copy in row_ins(g):
-            copy.wait_send()
-        col_in(g).wait_send()
-        col_back(g).wait_send()
-        row_back(g).wait_send()
+        for copy in (col_in, row_in, row_back, col_back):
+            copy(g).wait_send()
 
     for k in range(rounds):
         sum_copy(k).wait_send()
@@ -446,10 +443,11 @@
 ):
     tile_rows, fields, tile_cols, features = qkv.shape
     head_count = features // dim
-    heads = 2 if head_count % 2 == 0 else 1
+    heads = HEADS if head_count % HEADS == 0 else 1
     lanes = heads * dim
     chunks = head_count // heads
     half = win // 2
+    slots = half * tile_cols
     size = tile_rows * tile_cols
     pad = width * tile_rows
     rounds = sum(lax.axis_size(a).bit_length() - 1 for a in ("row", "col"))
@@ -480,26 +478,29 @@
         scratch_shapes=[
             vmem((chunks, tile_rows, fields, tile_cols, lanes), BF16),
             vmem((chunks, tile_rows, tile_cols, lanes), BF16),
-            vmem((chunks, half, fields, tile_cols, lanes), BF16),
-            vmem((chunks, half, tile_cols, lanes), BF16),
             vmem((chunks, 4, size - pad, lanes), BF16),
             vmem((chunks, 4, pad, lanes), BF16),
             vmem((chunks, 4, pad, lanes), BF16),
-            vmem((chunks, 4, size - pad, lanes), BF16),
+            vmem((chunks, 4, slots, lanes), BF16),
+            vmem((chunks, 4, slots, lanes), BF16),
+            vmem((chunks, 4, size, lanes), BF16),
+            vmem((chunks, 4, slots, lanes), BF16),
+            vmem((chunks, 4, slots, lanes), BF16),
             vmem((chunks, 4, pad, lanes), BF16),
             vmem((chunks, 4, pad, lanes), BF16),
-            vmem((chunks, half, 4, tile_cols, lanes), BF16),
-            vmem((chunks, half, 4, tile_cols, lanes), BF16),
             vmem((size, size), F32),
-            vmem((size, size + half * tile_cols), BF16),
             vmem((size, size), BF16),
+            vmem((slots, size), BF16),
+            vmem((size, size + slots), BF16),
+            vmem((slots, size), BF16),
+            vmem((pad, pad + slots), BF16),
+            vmem((size, size + slots), BF16),
             vmem((2, dim), F32),
             vmem((2 * size, size), F32),
             vmem((size, 2 * size), F32),
             vmem((2, head_count * 8, size), F32),
             vmem((rounds, sum_rows, 2 * size), F32),
             vmem((rounds, sum_rows, 2 * size), F32),
-            dma((2, chunks)),
             dma((2, chunks)),
             dma((2, chunks)),
             dma((2, chunks)),

time: 65.3 us -> 64.2 us (0.983)
  Pallas kernels: 57.3 us -> 56.1 us
    pallas_call x1, Pallas kernels: 57.3 us -> 56.1 us  [window_pass(): pl.pallas_call(functools.partial(window_kernel, row_dir=row_dir, col_dir=...]
where the time goes in v1:
time: 64.2 us; the launch traced here: 63.6 us
  Pallas kernels  56.1 us (87%)
  local copies, waits for them, and re-layouts  4.81 us (7%)
  between operations  1.95 us (3%)
  loops' own time  0.76 us (1%)
    pallas_call x1, Pallas kernels, window_pass(): pl.pallas_call(functools.partial(window_kernel, row_dir=row_dir, col_dir=...  56.1 us
    unnamed x4, local copies, waits for them, and re-layouts  3.5 us
    slice x1, local copies, waits for them, and re-layouts, local(): index = jnp.where(shifts[0] <= half, 0, win - 1) + shifts[1] - 1  1.31 us

profile of v1, /device:TPU:0, one launch (start us, length us, event | category | flops | bytes accessed | tf_op | source)
XLA Modules:
  0.0 63.6 jit_solution(8869987064828237273)
XLA Ops:
  0.6 1.3 %fusion = (s32[1]{0:T(128)}, s32[1]{0:T(128)}) fusion(s32[2]{0:T(128)} %param.24), kind=kLoop, calls=%fused_computation | loop fusion | bytes 16 | tf_op jit(solution)/shard_map/slice | solution.py:537
  3.2 56.9 %conditional.1 = ((bf16[16,8,3072]{2,1,0:T(8,128)(2,1)S(1)}, bf16[16,3,8,3072]{3,2,1,0:T(8,128)(2,1)S(1)}, f32[2,128]{1,0:T(2,128)S(1)}, f32[15,15,24]{2,1,0:T(8,128)S(1)})) conditional(s32[]{:T(128)} %bitcast, (s32[2]{0:T(128)}, bf16[16,3,8,3072]{3,2,1,0:T(8,128)(2,1)}, bf16[16,8,3072]{2,1,0:T(8,128)(2,1)}, ...), branch_computations={%region_0.1_spmd, %region_1.2_spmd, %region_2.3_spmd, %region_3.4_... | conditional | bytes 8 | solution.py:538
  3.5 56.1 %windows.20 = (bf16[16,8,3072]{2,1,0:T(8,128)(2,1)S(1)}, bf16[16,3,8,3072]{3,2,1,0:T(8,128)(2,1)S(1)}, f32[2,128]{1,0:T(2,128)S(1)}, f32[15,15,24]{2,1,0:T(8,128)S(1)}) custom-call(s32[2]{0:T(128)} %get-tuple-element.204.steps, bf16[16,3,8,3072]{3,2,1,0:T(8,128)(2,1)} %get-tuple-element.205.qkv, bf16[16,8,3072]{2,1,0:T(8,128)(2,1)} %get-tuple-element.206.cot, ...), custom_call_target="tpu_custom_call" | custom-call | tf_op jit(solution)/shard_map/cond/branch_6_fun/windows/pallas_call | solution.py:459
  60.1 0.9 %copy.70 = bf16[16,8,3072]{2,1,0:T(8,128)(2,1)} copy(bf16[16,8,3072]{2,1,0:T(8,128)(2,1)S(1)} %get-tuple-element.326) | data formatting | bytes 1572864
  61.0 1.4 %copy.71 = bf16[16,8,3,3072]{3,1,2,0:T(8,128)(2,1)} copy(bf16[16,8,3,3072]{3,1,2,0:T(8,128)(2,1)S(1)} %bitcast.48) | data formatting | bytes 4718592
  62.4 0.6 copy.72
  63.0 0.6 %copy.73 = f32[24,15,15]{0,2,1:T(8,128)} copy(f32[24,15,15]{0,2,1:T(8,128)S(1)} %bitcast.49) | data formatting | bytes 43200

commit v2 on v1

--- a/solution.py
+++ b/solution.py
@@ -14,8 +14,8 @@
 F32 = jnp.float32
 BF16 = jnp.bfloat16
 HEADS = 2
-LAG_COMPUTE = 3
-LAG_RETURN = 3
+LAG_COMPUTE = 4
+LAG_RETURN = 4
 LAG_FINAL = 4
 
 
@@ -280,39 +280,22 @@
     sub = 8
     lane_at = lax.broadcasted_iota(jnp.int32, (sub, size), 1)
 
-    def attend(g, i, fields):
-        at = head_lanes[i]
-        head = g * heads + i
-        q, k, v, ct = [field[:, i * dim : (i + 1) * dim] for field in fields]
-        q_hat, q_inv, qn = normed(q.astype(F32), gain_q)
-        k_hat, k_inv, kn = normed(k.astype(F32), gain_k)
+    def bias_of(head):
         base = jnp.broadcast_to(across_table[pl.ds(head, 1), :], (sub, 2 * size))
         base = pltpu.roll(base, 0, 1, stride=1, stride_axis=0)
         low, high = base[:, :size], base[:, size:]
-        blocks = []
-        for b in range(size // sub):
-            if b == 0:
-                blocks.append(low)
-            else:
-                blocks.append(
-                    jnp.where(
-                        lane_at < b * sub,
-                        pltpu.roll(high, b * sub, 1),
-                        pltpu.roll(low, b * sub, 1),
-                    )
+        blocks = [low]
+        for b in range(1, size // sub):
+            blocks.append(
+                jnp.where(
+                    lane_at < b * sub,
+                    pltpu.roll(high, b * sub, 1),
+                    pltpu.roll(low, b * sub, 1),
                 )
-        bias = jnp.concatenate(blocks, axis=0)
-        s = dot(qn, kn, 1, 1) * scale + bias + neg[...]
-        e = jnp.exp(s - jnp.max(s, axis=-1, keepdims=True))
-        p = e * (1.0 / jnp.sum(e, axis=-1, keepdims=True))
-        pb = p.astype(BF16)
-        att = dot(pb, v, 1, 0)
-        dp = dot(ct, v, 1, 1)
-        ds = p * (dp - jnp.sum(p * dp, axis=-1, keepdims=True))
-        dsb = ds.astype(BF16)
-        dqn = dot(dsb, kn, 1, 0) * scale
-        dkn = dot(dsb, qn, 0, 0) * scale
-        dv = dot(pb, ct, 0, 0)
+            )
+        return jnp.concatenate(blocks, axis=0)
+
+    def fold(head, ds):
         low, high = ds[:sub], jnp.zeros((sub, size), F32)
         for b in range(1, size // sub):
             moved = pltpu.roll(ds[b * sub : (b + 1) * sub], size - b * sub, 1)
@@ -321,11 +304,38 @@
             high = high + jnp.where(inside, 0.0, moved)
         skew[0, pl.ds(head * sub, sub), :] = low
         skew[1, pl.ds(head * sub, sub), :] = high
-        dq, gq = norm_back(q_hat, q_inv, dqn, gain_q)
-        dk, gk = norm_back(k_hat, k_inv, dkn, gain_k)
-        for f, value in enumerate((att, dq, dk, dv)):
-            results[g, f, :, at] = value.astype(BF16)
-        return jnp.concatenate([gq, gk], axis=0)
+
+    def softmax(s):
+        e = jnp.exp(s - jnp.max(s, axis=-1, keepdims=True))
+        return e * (1.0 / jnp.sum(e, axis=-1, keepdims=True))
+
+    def attend(g, fields):
+        each = range(heads)
+        split_heads = [[x[:, i * dim : (i + 1) * dim] for x in fields] for i in each]
+        q, k, v, ct = zip(*split_heads)
+        bias = [bias_of(g * heads + i) + neg[...] for i in each]
+        qs = [normed(x.astype(F32), gain_q) for x in q]
+        ks = [normed(x.astype(F32), gain_k) for x in k]
+        qn, kn = [x[2] for x in qs], [x[2] for x in ks]
+        s = [dot(qn[i], kn[i], 1, 1) for i in each]
+        dp = [dot(ct[i], v[i], 1, 1) for i in each]
+        p = [softmax(s[i] * scale + bias[i]) for i in each]
+        ds = [p[i] * (dp[i] - jnp.sum(p[i] * dp[i], axis=-1, keepdims=True)) for i in each]
+        pb = [x.astype(BF16) for x in p]
+        dsb = [x.astype(BF16) for x in ds]
+        dqn = [dot(dsb[i], kn[i], 1, 0) * scale for i in each]
+        dkn = [dot(dsb[i], qn[i], 0, 0) * scale for i in each]
+        att = [dot(pb[i], v[i], 1, 0) for i in each]
+        dv = [dot(pb[i], ct[i], 0, 0) for i in each]
+        total = 0.0
+        for i, at in enumerate(head_lanes):
+            fold(g * heads + i, ds[i])
+            dq, gq = norm_back(qs[i][0], qs[i][1], dqn[i], gain_q)
+            dk, gk = norm_back(ks[i][0], ks[i][1], dkn[i], gain_k)
+            for f, value in enumerate((att[i], dq, dk, dv[i])):
+                results[g, f, :, at] = value.astype(BF16)
+            total = total + jnp.concatenate([gq, gk], axis=0)
+        gain_sum[...] += total
 
     def compute(g):
         row_in(g).wait_recv()
@@ -334,8 +344,7 @@
             both = in_place(tokens[g, f], col_recv[g, f])
             both = jnp.concatenate([both, row_recv[g, f]], axis=0)
             fields.append(dot(gather[...], both, 1, 0).astype(BF16))
-        parts = [attend(g, i, fields) for i in range(heads)]
-        gain_sum[...] += functools.reduce(jnp.add, parts)
+        attend(g, fields)
         for f in range(4):
             row_out[g, f] = dot(strip_out[...], results[g, f], 1, 0).astype(BF16)
         row_back(g).start()

time: 64.2 us -> 55.6 us (0.87); the launches traced: 63.6 us -> 56.2 us
  Pallas kernels: 56.1 us -> 48.8 us
    pallas_call x1, Pallas kernels: 56.1 us -> 48.8 us  [window_pass(): pl.pallas_call(functools.partial(window_kernel, row_dir=row_dir, col_dir=...]
where the time goes in v2:
time: 55.6 us; the launch traced here: 56.2 us
  Pallas kernels  48.8 us (88%)
  local copies, waits for them, and re-layouts  4.81 us (9%)
  between operations  1.95 us (4%)
  loops' own time  0.57 us (1%)
    pallas_call x1, Pallas kernels, window_pass(): pl.pallas_call(functools.partial(window_kernel, row_dir=row_dir, col_dir=...  48.8 us
    unnamed x4, local copies, waits for them, and re-layouts  3.5 us
    slice x1, local copies, waits for them, and re-layouts, local(): index = jnp.where(shifts[0] <= half, 0, win - 1) + shifts[1] - 1  1.31 us

profile of v2, /device:TPU:0, one launch (start us, length us, event | category | flops | bytes accessed | tf_op | source)
XLA Modules:
  0.0 56.2 jit_solution(2795474133244033326)
XLA Ops:
  0.6 1.3 %fusion = (s32[1]{0:T(128)}, s32[1]{0:T(128)}) fusion(s32[2]{0:T(128)} %param.24), kind=kLoop, calls=%fused_computation | loop fusion | bytes 16 | tf_op jit(solution)/shard_map/slice | solution.py:546
  3.2 49.4 %conditional.1 = ((bf16[16,8,3072]{2,1,0:T(8,128)(2,1)S(1)}, bf16[16,3,8,3072]{3,2,1,0:T(8,128)(2,1)S(1)}, f32[2,128]{1,0:T(2,128)S(1)}, f32[15,15,24]{2,1,0:T(8,128)S(1)})) conditional(s32[]{:T(128)} %bitcast, (s32[2]{0:T(128)}, bf16[16,3,8,3072]{3,2,1,0:T(8,128)(2,1)}, bf16[16,8,3072]{2,1,0:T(8,128)(2,1)}, ...), branch_computations={%region_0.1_spmd, %region_1.2_spmd, %region_2.3_spmd, %region_3.4_... | conditional | bytes 8 | solution.py:547
  3.3 48.8 %windows.14 = (bf16[16,8,3072]{2,1,0:T(8,128)(2,1)S(1)}, bf16[16,3,8,3072]{3,2,1,0:T(8,128)(2,1)S(1)}, f32[2,128]{1,0:T(2,128)S(1)}, f32[15,15,24]{2,1,0:T(8,128)S(1)}) custom-call(s32[2]{0:T(128)} %get-tuple-element.168.steps, bf16[16,3,8,3072]{3,2,1,0:T(8,128)(2,1)} %get-tuple-element.169.qkv, bf16[16,8,3072]{2,1,0:T(8,128)(2,1)} %get-tuple-element.170.cot, ...), custom_call_target="tpu_custom_call" | custom-call | tf_op jit(solution)/shard_map/cond/branch_0_fun/windows/pallas_call | solution.py:468
  52.7 0.9 %copy.70 = bf16[16,8,3072]{2,1,0:T(8,128)(2,1)} copy(bf16[16,8,3072]{2,1,0:T(8,128)(2,1)S(1)} %get-tuple-element.326) | data formatting | bytes 1572864
  53.5 1.4 %copy.71 = bf16[16,8,3,3072]{3,1,2,0:T(8,128)(2,1)} copy(bf16[16,8,3,3072]{3,1,2,0:T(8,128)(2,1)S(1)} %bitcast.48) | data formatting | bytes 4718592
  54.9 0.6 %copy.72 = f32[2,128]{1,0:T(2,128)} copy(f32[2,128]{1,0:T(2,128)S(1)} %get-tuple-element.328) | data formatting | bytes 2048
  55.5 0.6 %copy.73 = f32[24,15,15]{0,2,1:T(8,128)} copy(f32[24,15,15]{0,2,1:T(8,128)S(1)} %bitcast.49) | data formatting | bytes 43200
